TPU v7x, 32 devices: a whole 2x2x4 slice. The times are simulated.
32 devices in a mesh: row: 4 (over z), col: 8 (over y, x, core).
Axes of the slice: x: 2, y: 2, z: 4, core: 2. Of those that a mesh axis runs over, the one named last changes fastest.
Arguments:
- neighbor: int32 [32, 3072, 3072], P(None, 'col', 'row'), may hold values from 0 to 1, as said below
- true_coords: float32 [32, 3, 3072], P(None, None, ('row', 'col')), as said below
- pred_coords: float32 [32, 3, 3072], P(None, None, ('row', 'col')), as said below
- residue_mask: int32 [32, 3072], P(None, ('row', 'col')), may hold values from 0 to 1, as said below
- single: bfloat16 [32, 3072, 384], P(None, ('row', 'col'))
- ln_gain: float32 [384], replicated, may hold values from 0.1 to 1.9
- w_hidden: bfloat16 [384, 128], replicated, may hold values from -0.3125 to 0.3125
- b_hidden: float32 [128], replicated, may hold values from -3 to 3
- w_mid: bfloat16 [128, 128], replicated, may hold values from -0.5 to 0.5
- b_mid: float32 [128], replicated, may hold values from -3 to 3
- w_logits: bfloat16 [128, 50], replicated, may hold values from -1.5 to 1.5
- b_logits: float32 [50], replicated, may hold values from -4 to 4
Outputs:
- lddt_score: float32 [32, 3072], P(None, ('row', 'col'))
- residue_loss: float32 [32, 3072], P(None, ('row', 'col'))
- total_loss: float32 [], replicated
Inputs may be any that keep to these rules, and one draw needn't show every extreme that they name: `neighbor`: 0 or 1; 0 where j == i; 1 wherever 0 < |i - j| <= 8. `residue_mask`: per structure, 1 on a leading run of 1536 or more residues and 0 after it. `true_coords`: positions in angstroms. `pred_coords`: positions in angstroms.
All inputs are finite; a program needn't handle non-finite values.
Results may differ from a plain program's by a relative error of at most 0.00098.
Values sent between devices are 32-bit elements; how exact they have to be, the bound alone decides.
A program may use at most 128 MiB of HBM per device.

v0:
```python
import jax
import jax.numpy as jnp
from jax import lax
from jax.sharding import PartitionSpec as P

L = 3072
THRESHOLDS = (0.5, 1.0, 2.0, 4.0)


def from_root(shard, axis, root):
    mine = lax.axis_index(axis) == root
    return lax.psum(jnp.where(mine, shard, jnp.zeros_like(shard)), axis)


def tile_dist(rows_block, cols_block):
    total = (cols_block[:, 0, :, None] - rows_block[:, 0, None, :]) ** 2
    total = total + (cols_block[:, 1, :, None] - rows_block[:, 1, None, :]) ** 2
    total = total + (cols_block[:, 2, :, None] - rows_block[:, 2, None, :]) ** 2
    return jnp.sqrt(total + 1e-10)


def head_loss(lddt_value, single, ln_gain, w_hidden, b_hidden, w_mid, b_mid, w_logits, b_logits):
    features = single.astype(jnp.float32)
    average = jnp.mean(features, axis=-1, keepdims=True)
    centred = features - average
    variance = jnp.mean(centred * centred, axis=-1, keepdims=True)
    normed = (centred * lax.rsqrt(variance + 1e-05) * ln_gain).astype(jnp.bfloat16)
    first_hidden = jax.nn.relu(
        jnp.dot(normed, w_hidden, preferred_element_type=jnp.float32) + b_hidden
    ).astype(jnp.bfloat16)
    second_hidden = jax.nn.relu(
        jnp.dot(first_hidden, w_mid, preferred_element_type=jnp.float32) + b_mid
    ).astype(jnp.bfloat16)
    logits = jnp.dot(second_hidden, w_logits, preferred_element_type=jnp.float32) + b_logits
    log_total = jnp.log(jnp.sum(jnp.exp(logits), axis=-1))
    bins = logits.shape[-1]
    centers = (jnp.arange(bins).astype(jnp.float32) + 0.5) / bins
    closeness = jnp.exp(-((lddt_value[..., None] - centers) ** 2) * (bins * bins * 0.5))
    target = closeness / jnp.sum(closeness, axis=-1, keepdims=True)
    return log_total - jnp.sum(target * logits, axis=-1)


def local(
    neighbor,
    true_coords,
    pred_coords,
    residue_mask,
    single,
    ln_gain,
    w_hidden,
    b_hidden,
    w_mid,
    b_mid,
    w_logits,
    b_logits,
):
    valid = residue_mask.astype(jnp.float32)
    own_len = residue_mask.shape[1]
    stacked = jnp.concatenate([true_coords, pred_coords, valid[:, None, :]], axis=1)
    row_count = lax.axis_size("row")
    col_count = lax.axis_size("col")
    rows_len = L // row_count
    cols_len = L // col_count
    col_index = lax.axis_index("col")
    rows_part = lax.all_gather(stacked, "col", axis=2, tiled=True)
    offset = col_index * cols_len % rows_len
    column_piece = lax.dynamic_slice_in_dim(rows_part, offset, cols_len, 2)
    source_row = col_index * cols_len // rows_len
    cols_part = from_root(column_piece, "row", source_row)
    true_dist = tile_dist(rows_part[:, 0:3], cols_part[:, 0:3])
    pred_dist = tile_dist(rows_part[:, 3:6], cols_part[:, 3:6])
    mismatch = jnp.abs(pred_dist - true_dist)
    scores = jnp.zeros_like(mismatch)
    for threshold in THRESHOLDS:
        scores = scores + jax.nn.sigmoid(4.0 * (threshold - mismatch))
    scores = 0.25 * scores
    weights = neighbor.astype(jnp.float32) * rows_part[:, 6, None, :] * cols_part[:, 6, :, None]
    preserved = jnp.sum(weights * scores, axis=1)
    neighbors = jnp.sum(weights, axis=1)
    preserved_all, neighbors_all = lax.psum((preserved, neighbors), "col")
    preserved_own = lax.dynamic_slice_in_dim(preserved_all, col_index * own_len, own_len, 1)
    neighbors_own = lax.dynamic_slice_in_dim(neighbors_all, col_index * own_len, own_len, 1)
    lddt_score = preserved_own / jnp.maximum(neighbors_own, 1.0)
    residue_loss = valid * head_loss(
        lddt_score, single, ln_gain, w_hidden, b_hidden, w_mid, b_mid, w_logits, b_logits
    )
    loss_sum, valid_sum = lax.psum((jnp.sum(residue_loss), jnp.sum(valid)), ("row", "col"))
    total_loss = loss_sum / valid_sum
    return (lddt_score, residue_loss, total_loss)


def solution(mesh):
    placed = (
        P(None, "col", "row"),
        P(None, None, ("row", "col")),
        P(None, None, ("row", "col")),
        P(None, ("row", "col")),
        P(None, ("row", "col"), None),
        P(),
        P(),
        P(),
        P(),
        P(),
        P(),
        P(),
    )
    return jax.shard_map(
        local,
        mesh=mesh,
        in_specs=placed,
        out_specs=(P(None, ("row", "col")), P(None, ("row", "col")), P()),
        check_vma=False,
    )
```

profile of v0, /device:TPU:0, one launch (start us, length us, event | category | flops | bytes accessed | tf_op | source)
XLA Modules:
  0.0 312.7 jit_solution(15335422747212448188)
XLA Ops:
  7.2 0.0 copy-start
  7.2 0.0 all-reduce.5.cloned.1.call-start
  7.3 0.7 convert_bitcast_fusion
  8.0 0.8 pad_maximum_fusion
  8.8 0.9 copy.33
  9.7 21.3 %all_gather.3 = f32[32,7,768]{0,1,2:T(8,128)S(1)} all-gather(f32[32,7,96]{0,1,2:T(8,128)} %copy.33), channel_id=1, replica_groups=mesh['row'=4,'col'=8] {'col'}, dimensions={2}, use_global_device_ids=true | all-gather | bytes 774144 | tf_op jit(solution)/shard_map/all_gather | solution.py:65
  31.0 1.3 dynamic-slice_select_fusion
  32.3 0.0 all-reduce.5.cloned.1.call-update
  32.3 0.0 all-reduce.7.cloned.1.call-start
  32.4 3.3 %fusion.31 = (f32[32,1,768]{0,1,2:T(1,128)}, f32[32,1,768]{0,1,2:T(1,128)}, f32[32,1,768]{0,1,2:T(1,128)}, f32[32,1,768]{0,1,2:T(1,128)}, f32[32,1,768]{0,1,2:T(...) fusion(f32[32,7,768]{0,1,2:T(8,128)S(1)} %all_gather.3), kind=kLoop, calls=%fused_computation.43 | loop fusion | bytes 1376256 | tf_op jit(solution)/shard_map/slice | solution.py:77
  35.6 2.3 convert_reduce_fusion
  37.9 2.8 fusion.4
  40.8 0.0 copy-done
  40.8 3.2 %maximum_convert_fusion = bf16[32,96,128]{2,1,0:T(8,128)(2,1)S(1)} fusion(bf16[32,96,384]{2,1,0:T(8,128)(2,1)} %param.16, f32[384]{0:T(512)} %param.17, f32[32,96]{1,0:T(8,128)S(1)} %add_rsqrt_fusion, f32[32,96]{1,0:T(8,128)S(1)} %broadcast_multiply_fusion, f32[128]{0:T(128)} %param.21, f32[128]{0:T(128)} %param.19, bf16[384,128]{1,0:T(8,128)(2,1)S(1)} %copy-done, ...), kind=kOutput, calls=%fused_computation.15 | convolution fusion | flops 410910720 | bytes 3303936 | tf_op jit(solution)/shard_map/dot_general | solution.py:32
  44.0 1.1 copy.34
  45.1 1.1 copy.37
  46.2 1.1 copy.39
  47.4 1.1 copy.41
  48.5 1.1 copy.43
  49.7 1.1 copy.45
  50.8 1.1 copy.47
  51.9 1.4 exponential_reduce_fusion
  53.4 48.4 %all-reduce.5.cloned.1.call-done = f32[32,7,384]{0,1,2:T(8,128)} async-done(((f32[32,7,384]{0,1,2:T(8,128)}), f32[32,7,384]{0,1,2:T(8,128)}) %all-reduce.5.cloned.1.call-update) | async-done | bytes 344080 | tf_op jit(solution)/shard_map/psum | solution.py:12
  101.7 6.8 %fusion.32 = (f32[32,1,384]{0,1,2:T(1,128)S(1)}, f32[32,1,384]{0,1,2:T(1,128)S(1)}, f32[32,1,384]{0,1,2:T(1,128)S(1)}, f32[32,1,384]{0,1,2:T(1,128)S(1)}, f32[32...) fusion(f32[32,7,384]{0,1,2:T(8,128)} %all-reduce.5.cloned.1.call-done), kind=kLoop, calls=%fused_computation.44 | loop fusion | bytes 688128 | tf_op jit(solution)/shard_map/slice | solution.py:77
  108.5 0.1 copy.35
  108.6 0.1 copy.36
  108.7 0.1 copy.38
  108.8 0.1 copy.40
  108.9 0.1 copy.42
  109.1 0.1 copy.44
  109.2 0.1 copy.46
  109.3 0.0 copy-start.1
  109.3 98.8 %multiply_reduce_fusion = (f32[32,768]{1,0:T(8,128)}, f32[32,768]{1,0:T(8,128)}) fusion(s32[32,384,768]{2,1,0:T(8,128)} %param.12, f32[32,768]{1,0:T(8,128)S(1)} %copy.47, f32[32,384]{1,0:T(8,128)S(1)} %copy.46, f32[32,768]{1,0:T(8,128)S(1)} %copy.45, f32[32,384]{1,0:T(8,128)S(1)} %copy.44, f32[32,768]{1,0:T(8,128)S(1)} %copy.43, f32[32,384]{1,0:T(8,128)S(1)} %copy.42, ...), kind=kLoop, calls=%fused_computation.1 | loop fusion | flops 471810048 | bytes 38977536 | tf_op jit(solution)/shard_map/reduce_sum | solution.py:78
  208.1 0.0 all-reduce.7.cloned.1.call-update
  208.2 53.1 %all-reduce.7.cloned.1.call-done = (f32[32,768]{1,0:T(8,128)}, f32[32,768]{1,0:T(8,128)}) async-done(((f32[32,768]{1,0:T(8,128)}, f32[32,768]{1,0:T(8,128)}), (f32[32,768]{1,0:T(8,128)}, f32[32,768]{1,0:T(8,128)})) %all-reduce.7.cloned.1.call-update) | async-done | bytes 196624 | tf_op jit(solution)/shard_map/psum | solution.py:80
  261.3 0.9 maximum_divide_fusion
  262.1 0.0 copy-start.2
  262.1 0.4 fusion.33
  262.6 0.0 copy-done.1
  262.6 1.3 fusion.30
  263.9 39.6 %all-reduce = (f32[]{:T(128)}, f32[]{:T(128)}) all-reduce(f32[]{:T(128)} %get-tuple-element.12, f32[]{:T(128)} %get-tuple-element.28), channel_id=1, replica_groups=mesh['row'=4,'col'=8] {'row','col'}, use_global_device_ids=true, to_apply=%region_11.12 | all-reduce | flops 2 | bytes 16 | tf_op jit(solution)/shard_map/psum | solution.py:87
  304.7 0.0 copy-done.2
  (3 shorter events, 0.0 us)
Async XLA Ops:
  7.2 33.6 %copy-start = (bf16[384,128]{1,0:T(8,128)(2,1)S(1)}, bf16[384,128]{1,0:T(8,128)(2,1)}, u32[]{:S(2)}) copy-start(bf16[384,128]{1,0:T(8,128)(2,1)} %param.18) | copy-start | bytes 294916
  7.2 94.6 %all-reduce.5.cloned.1.call-start = ((), (), s32[]{:S(2)}) async-start(), calls=%async_computation | async-start | bytes 3145728 | tf_op jit(solution)/shard_map/psum | solution.py:12
  32.3 228.9 %all-reduce.7.cloned.1.call-start = ((), (), s32[]{:S(2)}) async-start(), calls=%async_computation.1 | async-start | bytes 393216 | tf_op jit(solution)/shard_map/psum | solution.py:80
  109.3 153.3 %copy-start.1 = (s32[32,96]{1,0:T(8,128)S(1)}, s32[32,96]{1,0:T(8,128)}, u32[]{:S(2)}) copy-start(s32[32,96]{1,0:T(8,128)} %param.15) | copy-start | bytes 36868
  262.1 42.6 %copy-start.2 = (f32[32,96]{1,0:T(8,128)}, f32[32,96]{1,0:T(8,128)S(1)}, u32[]{:S(2)}) copy-start(f32[32,96]{1,0:T(8,128)S(1)} %maximum_divide_fusion) | copy-start | bytes 36868
Sparse Core Ops, SparseCore 0:
  32.5 69.2 all-reduce.4
  208.3 52.9 all-reduce.6
where the time goes:
time: 314 us; the launch traced here: 313 us
  other arithmetic  109 us (35%)
  waiting for transfers between devices  102 us (32%)
  blocking collectives  60.8 us (19%)
  local copies, waits for them, and re-layouts  19.7 us (6%)
  between operations  16.6 us (5%)
  matrix products  4.59 us (1%)
    reduce_sum x1, other arithmetic, local(): preserved = jnp.sum(weights * scores, axis=1)  98.8 us
    psum x1, waiting for transfers between devices, local(): preserved_all, neighbors_all = lax.psum((preserved, neighbors), 'col')  53.1 us
    psum x1, waiting for transfers between devices, from_root(): return lax.psum(jnp.where(mine, shard, jnp.zeros_like(shard)), axis)  48.4 us
    psum x1, blocking collectives, local(): lax.psum((jnp.sum(residue_loss), jnp.sum(valid)), ('row', 'col'))  39.6 us
    all_gather x1, blocking collectives, local(): rows_part = lax.all_gather(stacked, 'col', axis=2, tiled=True)  21.3 us
    slice x1, local copies, waits for them, and re-layouts, local(): cols_part[:, 6, :, None]  6.78 us
  transfers between devices with their start and end apart: 2, of which 2 were waited for; matrix products, arithmetic and copies ran while one was open for 7% of the time, Pallas kernels for 0%

commit v1 on v0

--- a/solution.py
+++ b/solution.py
@@ -84,7 +84,7 @@
     residue_loss = valid * head_loss(
         lddt_score, single, ln_gain, w_hidden, b_hidden, w_mid, b_mid, w_logits, b_logits
     )
-    loss_sum, valid_sum = lax.psum((jnp.sum(residue_loss), jnp.sum(valid)), ("row", "col"))
+    loss_sum, valid_sum = lax.psum(lax.psum((jnp.sum(residue_loss), jnp.sum(valid)), "col"), "row")
     total_loss = loss_sum / valid_sum
     return (lddt_score, residue_loss, total_loss)
 

time: 314 us -> 299 us (0.952)
  blocking collectives: 60.8 us -> 46.1 us
    psum x1 -> x2, blocking collectives: 39.6 us -> 24.8 us  [the longest x1 12.5 us: local(): lax.psum((jnp.sum(residue_loss), jnp.sum(valid)), 'col')]
where the time goes in v1:
time: 299 us; the launch traced here: 298 us
  other arithmetic  109 us (36%)
  waiting for transfers between devices  102 us (34%)
  blocking collectives  46.1 us (15%)
  local copies, waits for them, and re-layouts  19.7 us (7%)
  between operations  16.6 us (6%)
  matrix products  4.59 us (2%)
    reduce_sum x1, other arithmetic, local(): preserved = jnp.sum(weights * scores, axis=1)  98.8 us
    psum x1, waiting for transfers between devices, local(): preserved_all, neighbors_all = lax.psum((preserved, neighbors), 'col')  53.1 us
    psum x1, waiting for transfers between devices, from_root(): return lax.psum(jnp.where(mine, shard, jnp.zeros_like(shard)), axis)  48.4 us
    all_gather x1, blocking collectives, local(): rows_part = lax.all_gather(stacked, 'col', axis=2, tiled=True)  21.3 us
    psum x1, blocking collectives, local(): lax.psum((jnp.sum(residue_loss), jnp.sum(valid)), 'col')  12.5 us
    psum x1, blocking collectives, local(): lax.psum(lax.psum((jnp.sum(residue_loss), jnp.sum(valid)), 'col'), 'row')  12.3 us
    slice x1, local copies, waits for them, and re-layouts, local(): cols_part[:, 6, :, None]  6.78 us
  transfers between devices with their start and end apart: 2, of which 2 were waited for; matrix products, arithmetic and copies ran while one was open for 7% of the time, Pallas kernels for 0%

profile of v1, /device:TPU:0, one launch (start us, length us, event | category | flops | bytes accessed | tf_op | source)
XLA Modules:
  0.0 297.8 jit_solution(2416281162743364807)
XLA Ops:
  7.2 0.0 copy-start
  7.2 0.0 all-reduce.6.cloned.1.call-start
  7.3 0.7 convert_bitcast_fusion
  8.0 0.8 pad_maximum_fusion
  8.8 0.9 copy.33
  9.7 21.3 %all_gather.3 = f32[32,7,768]{0,1,2:T(8,128)S(1)} all-gather(f32[32,7,96]{0,1,2:T(8,128)} %copy.33), channel_id=1, replica_groups=mesh['row'=4,'col'=8] {'col'}, dimensions={2}, use_global_device_ids=true | all-gather | bytes 774144 | tf_op jit(solution)/shard_map/all_gather | solution.py:65
  31.0 1.3 dynamic-slice_select_fusion
  32.3 0.0 all-reduce.6.cloned.1.call-update
  32.3 0.0 all-reduce.8.cloned.1.call-start
  32.4 3.3 %fusion.31 = (f32[32,1,768]{0,1,2:T(1,128)}, f32[32,1,768]{0,1,2:T(1,128)}, f32[32,1,768]{0,1,2:T(1,128)}, f32[32,1,768]{0,1,2:T(1,128)}, f32[32,1,768]{0,1,2:T(...) fusion(f32[32,7,768]{0,1,2:T(8,128)S(1)} %all_gather.3), kind=kLoop, calls=%fused_computation.43 | loop fusion | bytes 1376256 | tf_op jit(solution)/shard_map/slice | solution.py:77
  35.6 2.3 convert_reduce_fusion
  37.9 2.8 fusion.4
  40.8 0.0 copy-done
  40.8 3.2 %maximum_convert_fusion = bf16[32,96,128]{2,1,0:T(8,128)(2,1)S(1)} fusion(bf16[32,96,384]{2,1,0:T(8,128)(2,1)} %param.16, f32[384]{0:T(512)} %param.17, f32[32,96]{1,0:T(8,128)S(1)} %add_rsqrt_fusion, f32[32,96]{1,0:T(8,128)S(1)} %broadcast_multiply_fusion, f32[128]{0:T(128)} %param.21, f32[128]{0:T(128)} %param.19, bf16[384,128]{1,0:T(8,128)(2,1)S(1)} %copy-done, ...), kind=kOutput, calls=%fused_computation.15 | convolution fusion | flops 410910720 | bytes 3303936 | tf_op jit(solution)/shard_map/dot_general | solution.py:32
  44.0 1.1 copy.34
  45.1 1.1 copy.37
  46.2 1.1 copy.39
  47.4 1.1 copy.41
  48.5 1.1 copy.43
  49.7 1.1 copy.45
  50.8 1.1 copy.47
  51.9 1.4 exponential_reduce_fusion
  53.4 48.4 %all-reduce.6.cloned.1.call-done = f32[32,7,384]{0,1,2:T(8,128)} async-done(((f32[32,7,384]{0,1,2:T(8,128)}), f32[32,7,384]{0,1,2:T(8,128)}) %all-reduce.6.cloned.1.call-update) | async-done | bytes 344080 | tf_op jit(solution)/shard_map/psum | solution.py:12
  101.7 6.8 %fusion.32 = (f32[32,1,384]{0,1,2:T(1,128)S(1)}, f32[32,1,384]{0,1,2:T(1,128)S(1)}, f32[32,1,384]{0,1,2:T(1,128)S(1)}, f32[32,1,384]{0,1,2:T(1,128)S(1)}, f32[32...) fusion(f32[32,7,384]{0,1,2:T(8,128)} %all-reduce.6.cloned.1.call-done), kind=kLoop, calls=%fused_computation.44 | loop fusion | bytes 688128 | tf_op jit(solution)/shard_map/slice | solution.py:77
  108.5 0.1 copy.35
  108.6 0.1 copy.36
  108.7 0.1 copy.38
  108.8 0.1 copy.40
  108.9 0.1 copy.42
  109.1 0.1 copy.44
  109.2 0.1 copy.46
  109.3 0.0 copy-start.1
  109.3 98.8 %multiply_reduce_fusion = (f32[32,768]{1,0:T(8,128)}, f32[32,768]{1,0:T(8,128)}) fusion(s32[32,384,768]{2,1,0:T(8,128)} %param.12, f32[32,768]{1,0:T(8,128)S(1)} %copy.47, f32[32,384]{1,0:T(8,128)S(1)} %copy.46, f32[32,768]{1,0:T(8,128)S(1)} %copy.45, f32[32,384]{1,0:T(8,128)S(1)} %copy.44, f32[32,768]{1,0:T(8,128)S(1)} %copy.43, f32[32,384]{1,0:T(8,128)S(1)} %copy.42, ...), kind=kLoop, calls=%fused_computation.1 | loop fusion | flops 471810048 | bytes 38977536 | tf_op jit(solution)/shard_map/reduce_sum | solution.py:78
  208.1 0.0 all-reduce.8.cloned.1.call-update
  208.2 53.1 %all-reduce.8.cloned.1.call-done = (f32[32,768]{1,0:T(8,128)}, f32[32,768]{1,0:T(8,128)}) async-done(((f32[32,768]{1,0:T(8,128)}, f32[32,768]{1,0:T(8,128)}), (f32[32,768]{1,0:T(8,128)}, f32[32,768]{1,0:T(8,128)})) %all-reduce.8.cloned.1.call-update) | async-done | bytes 196624 | tf_op jit(solution)/shard_map/psum | solution.py:80
  261.3 0.9 maximum_divide_fusion
  262.1 0.0 copy-start.2
  262.1 0.4 fusion.33
  262.6 0.0 copy-done.1
  262.6 1.2 fusion.30
  263.8 12.5 %all-reduce = (f32[]{:T(128)}, f32[]{:T(128)}) all-reduce(f32[]{:T(128)} %get-tuple-element.14, f32[]{:T(128)} %get-tuple-element.30), channel_id=1, replica_groups=mesh['row'=4,'col'=8] {'col'}, use_global_device_ids=true, to_apply=%region_11.12 | all-reduce | flops 2 | bytes 16 | tf_op jit(solution)/shard_map/psum | solution.py:87
  276.3 12.3 %all-reduce.2 = (f32[]{:T(128)}, f32[]{:T(128)}) all-reduce(f32[]{:T(128)} %get-tuple-element.8, f32[]{:T(128)} %get-tuple-element.9), channel_id=1, replica_groups=mesh['row'=4,'col'=8] {'row'}, use_global_device_ids=true, to_apply=%region_12.13 | all-reduce | flops 2 | bytes 16 | tf_op jit(solution)/shard_map/psum | solution.py:87
  289.9 0.0 copy-done.2
  (3 shorter events, 0.0 us)
Async XLA Ops:
  7.2 33.6 %copy-start = (bf16[384,128]{1,0:T(8,128)(2,1)S(1)}, bf16[384,128]{1,0:T(8,128)(2,1)}, u32[]{:S(2)}) copy-start(bf16[384,128]{1,0:T(8,128)(2,1)} %param.18) | copy-start | bytes 294916
  7.2 94.6 %all-reduce.6.cloned.1.call-start = ((), (), s32[]{:S(2)}) async-start(), calls=%async_computation | async-start | bytes 3145728 | tf_op jit(solution)/shard_map/psum | solution.py:12
  32.3 228.9 %all-reduce.8.cloned.1.call-start = ((), (), s32[]{:S(2)}) async-start(), calls=%async_computation.1 | async-start | bytes 393216 | tf_op jit(solution)/shard_map/psum | solution.py:80
  109.3 153.3 %copy-start.1 = (s32[32,96]{1,0:T(8,128)S(1)}, s32[32,96]{1,0:T(8,128)}, u32[]{:S(2)}) copy-start(s32[32,96]{1,0:T(8,128)} %param.15) | copy-start | bytes 36868
  262.1 27.7 %copy-start.2 = (f32[32,96]{1,0:T(8,128)}, f32[32,96]{1,0:T(8,128)S(1)}, u32[]{:S(2)}) copy-start(f32[32,96]{1,0:T(8,128)S(1)} %maximum_divide_fusion) | copy-start | bytes 36868
Sparse Core Ops, SparseCore 0:
  32.5 69.2 all-reduce.5
  208.3 52.9 all-reduce.7
